TPU v7x, 512 devices: a 8x2x16 block of a 8x8x16 slice. The times are simulated.
512 devices in a mesh: groups: 2 (over y), ctx: 32 (over z, core), tp: 8 (over x).
Axes of the slice: x: 8, y: 2, z: 16, core: 2. Of those that a mesh axis runs over, the one named last changes fastest.
The devices are a block of a 8x8x16 slice.
Arguments:
- q_nope: bfloat16 [4096, 16384], P(('groups', 'ctx'), 'tp'), parts along dimension 0, may hold values from -6 to 6
- q_rope: bfloat16 [4096, 8192], P(('groups', 'ctx'), 'tp'), parts along dimension 0, may hold values from -6 to 6
- c_kv: bfloat16 [4096, 512], P(('groups', 'ctx')), parts along dimension 0, may hold values from -6 to 46.4
- k_rope: bfloat16 [4096, 64], P(('groups', 'ctx')), parts along dimension 0, may hold values from -6 to 6
- positions: int32 [4096], P(('groups', 'ctx')), parts along dimension 0, may hold values from 0 to 2047, as said below
- w_uk: bfloat16 [128, 128, 512], P('tp', 'ctx'), may hold values from -0.5 to 0.5
- w_uv: bfloat16 [128, 512, 128], P('tp', 'ctx'), may hold values from -0.25 to 0.25
- w_out: bfloat16 [16384, 7168], P('tp', 'ctx'), may hold values from -0.125 to 0.125
Outputs:
- attn_proj: bfloat16 [4096, 7168], P(('groups', 'tp'), 'ctx'), parts along dimension 0
There are 2 independent parts, one for each index of `groups`. A program takes and returns all parts, laid end to end along the dimension named above; an argument that names none is the same for every part. Nothing has to cross between parts.
Inputs may be any that keep to these rules, and one draw needn't show every extreme that they name: The positions are the 2048 integers 0 to 2047, each once; every aligned block of 32 rows holds consecutive ascending positions.
All inputs are finite; a program needn't handle non-finite values.
Results may differ from a plain program's by a relative error of at most 0.015.
Values may be sent and summed in bfloat16 or wider, within the bound.
No kernel may reach another device: no remote copies, remote signals or barrier semaphores. Data moves between devices by JAX's collectives and lax.ppermute only.
A program may use at most 64 MiB of HBM per device.

v0:
```python
import jax
import jax.numpy as jnp
from jax import lax
from jax.sharding import PartitionSpec as P


def laid_out(blocks, dim):
    blocks = jnp.moveaxis(blocks, 0, dim)
    lengths = blocks.shape
    return blocks.reshape(*lengths[:dim], lengths[dim] * lengths[dim + 1], *lengths[dim + 2 :])


def gather_together(arrays, axis, dims):
    flat = jnp.concatenate([a.reshape(-1) for a in arrays])
    lines, at, gathered = (lax.all_gather(flat, axis), 0, [])
    for a, dim in zip(arrays, dims):
        blocks = lines[:, at : at + a.size].reshape(-1, *a.shape)
        gathered.append(laid_out(blocks, dim))
        at += a.size
    return tuple(gathered)


def in_blocks(x, dim, size):
    before, after = (x.shape[:dim], x.shape[dim + 1 :])
    return jnp.moveaxis(x.reshape(*before, size, -1, *after), dim, 0)


def sent_and_summed(x, axis, dim):
    blocks = in_blocks(x, dim, lax.axis_size(axis))
    arrived = lax.all_to_all(blocks, axis, split_axis=0, concat_axis=0, tiled=True)
    return arrived.astype(jnp.float32).sum(axis=0)


def rotate(values, position):
    half_dim = values.shape[-1] // 2
    freqs = 10000.0 ** (-jnp.arange(half_dim, dtype=jnp.float32) / half_dim)
    angles = position.astype(jnp.float32)[..., None] * freqs
    cosine = jnp.cos(angles)
    sine = jnp.sin(angles)
    first_half = values[..., :half_dim].astype(jnp.float32)
    second_half = values[..., half_dim:].astype(jnp.float32)
    return jnp.concatenate(
        [first_half * cosine - second_half * sine, second_half * cosine + first_half * sine],
        axis=-1,
    )


def on_device(q_nope, q_rope, c_kv, k_rope, positions, w_uk, w_uv, w_out):
    tok_count = q_nope.shape[0]
    head_count = w_uk.shape[0]
    latent = c_kv.shape[1]
    up_key, up_value = gather_together((w_uk, w_uv), "ctx", (1, 1))
    nope_dim = up_key.shape[1]
    rope_dim = k_rope.shape[1]
    softmax_scale = (nope_dim + rope_dim) ** (-0.5)
    q_parts = q_nope.reshape(tok_count, head_count, nope_dim)
    q_lat = jnp.einsum("thn,hnl->thl", q_parts, up_key, preferred_element_type=jnp.float32).astype(
        jnp.bfloat16
    )
    q_rot = rotate(q_rope.reshape(tok_count, head_count, rope_dim), positions[:, None]).astype(
        jnp.bfloat16
    )
    k_rot = rotate(k_rope, positions).astype(jnp.bfloat16)
    key_rows = jnp.concatenate([c_kv, k_rot], axis=1)
    queries = jnp.concatenate([q_lat, q_rot], axis=2).reshape(
        tok_count * head_count, latent + rope_dim
    )
    query_pos = jnp.repeat(positions, head_count)
    row_total = tok_count * head_count
    key_part = lax.all_gather(key_rows, "ctx", axis=0, tiled=True)
    key_pos = lax.all_gather(positions, "ctx", axis=0, tiled=True)
    run_max = jnp.full((row_total,), -1e30, jnp.float32)
    scores = (
        jnp.einsum("rk,sk->rs", queries, key_part, preferred_element_type=jnp.float32)
        * softmax_scale
    )
    visible = key_pos[None, :] <= query_pos[:, None]
    new_max = jnp.maximum(run_max, jnp.max(jnp.where(visible, scores, -1e30), axis=1))
    weights = jnp.where(visible, jnp.exp(scores - new_max[:, None]), 0.0)
    new_sum = jnp.sum(weights, axis=1)
    added = jnp.dot(
        weights.astype(jnp.bfloat16), key_part[:, :latent], preferred_element_type=jnp.float32
    )
    o_lat = (added / new_sum[:, None]).astype(jnp.bfloat16).reshape(tok_count, head_count, latent)
    head_out = jnp.einsum("thl,hlv->thv", o_lat, up_value, preferred_element_type=jnp.float32)
    rows_out = head_out.astype(jnp.bfloat16).reshape(tok_count, -1)
    partial_value = jnp.dot(
        lax.all_gather(rows_out, "ctx", axis=0, tiled=True),
        w_out,
        preferred_element_type=jnp.float32,
    )
    summed = sent_and_summed(partial_value.astype(jnp.bfloat16), "tp", 0)
    return summed.astype(jnp.bfloat16)


def solution(mesh):
    in_specs = (
        P(("groups", "ctx"), "tp"),
        P(("groups", "ctx"), "tp"),
        P(("groups", "ctx"), None),
        P(("groups", "ctx"), None),
        P(("groups", "ctx")),
        P("tp", "ctx", None),
        P("tp", "ctx", None),
        P("tp", "ctx"),
    )
    out_specs = P(("groups", "tp"), "ctx")
    return jax.shard_map(
        on_device, mesh=mesh, in_specs=in_specs, out_specs=out_specs, check_vma=False
    )
```

profile of v0, /device:TPU:65, one launch (start us, length us, event | category | flops | bytes accessed | tf_op | source)
XLA Modules:
  0.0 328.4 jit_solution(10513221402875094891)
XLA Ops:
  6.6 0.9 copy.33
  7.5 1.5 pad_maximum_fusion.1
  9.8 1.0 fusion.20
  10.8 1.6 pad_maximum_fusion.2
  12.5 1.3 dynamic-slice
  14.5 0.9 dynamic-update-slice
  15.4 57.5 %all-reduce = s32[2048]{0:T(1024)S(1)} all-reduce(s32[2048]{0:T(1024)S(1)} %dynamic-update-slice), channel_id=1, replica_groups=mesh['groups'=2,'ctx'=32,'tp'=8] {'ctx'}, use_global_device_ids=true, to_apply=%add | all-reduce | flops 2048 | bytes 16384
  73.7 1.1 reshape.118
  75.2 45.3 %all-gather.9.cloned.1.call-done = bf16[2097152]{0:T(1024)(128)(2,1)} async-done(((bf16[65536]{0:T(1024)(128)(2,1)}), bf16[2097152]{0:T(1024)(128)(2,1)}) %all-gather.9.cloned.1.call-update) | async-done | bytes 4194320 | tf_op jit(solution)/shard_map/all_gather | solution.py:15
  120.4 5.6 %reshape.123 = bf16[32,65536]{1,0:T(8,128)(2,1)} reshape(bf16[2097152]{0:T(1024)(128)(2,1)} %all-gather.9.cloned.1.call-done) | data formatting | bytes 8388608 | tf_op jit(solution)/shard_map/all_gather | solution.py:15
  126.0 4.4 %fusion.25 = (bf16[32,32768]{1,0:T(8,128)(2,1)}, bf16[4,8,256,128]{3,1,2,0:T(8,128)(2,1)}) fusion(bf16[32,65536]{1,0:T(8,128)(2,1)} %reshape.123), kind=kLoop, calls=%fused_computation.44 | loop fusion | bytes 8388608 | tf_op jit(solution)/shard_map/slice | solution.py:17
  130.4 3.3 %reshape.115 = bf16[32,16,4,512]{3,2,1,0:T(4,128)(2,1)S(1)} reshape(bf16[32,32768]{1,0:T(8,128)(2,1)} %get-tuple-element.5) | data formatting | bytes 4194304 | tf_op jit(solution)/shard_map/reshape | solution.py:17
  133.8 2.3 copy.20
  136.1 2.5 reshape.116
  138.6 1.4 fusion.6
  140.3 1.8 copy.24
  143.1 49.6 %all-gather.5.cloned.1.call-done = bf16[2048,576]{1,0:T(8,128)(2,1)} async-done(((bf16[64,576]{1,0:T(8,128)(2,1)}), bf16[2048,576]{1,0:T(8,128)(2,1)}) %all-gather.5.cloned.1.call-update) | async-done | bytes 2359312 | tf_op jit(solution)/shard_map/all_gather | solution.py:70
  192.8 5.9 %fusion = (f32[1024]{0:T(1024)S(1)}, f32[1024,2048]{1,0:T(8,128)S(1)}) fusion(s32[2048]{0:T(1024)S(1)} %all-reduce, s32[1024]{0:T(1024)S(1)} %le.16, bf16[1024,576]{1,0:T(8,128)(2,1)} %bitcast.43, bf16[2048,576]{1,0:T(8,128)(2,1)} %all-gather.5.cloned.1.call-done), kind=kOutput, calls=%fused_computation.2 | convolution fusion | flops 2424306688 | bytes 11943936 | tf_op jit(solution)/shard_map/rk,sk->rs/dot_general | solution.py:74
  198.7 2.8 fusion.1
  201.5 2.5 divide_convert_fusion
  204.0 1.4 fusion.7
  206.3 77.1 %all-gather.7.cloned.1.call-done = bf16[2048,2048]{1,0:T(8,128)(2,1)} async-done(((bf16[64,2048]{1,0:T(8,128)(2,1)}), bf16[2048,2048]{1,0:T(8,128)(2,1)}) %all-gather.7.cloned.1.call-update) | async-done | bytes 8388624 | tf_op jit(solution)/shard_map/all_gather | solution.py:88
  283.4 6.0 %convolution_convert_fusion = bf16[2048,224]{0,1:T(8,128)(2,1)S(1)} fusion(bf16[2048,2048]{1,0:T(8,128)(2,1)} %all-gather.7.cloned.1.call-done, bf16[2048,224]{0,1:T(8,128)(2,1)S(1)} %copy-done), kind=kOutput, calls=%fused_computation.6 | convolution fusion | flops 1879506944 | bytes 10223616 | tf_op jit(solution)/shard_map/dot_general | solution.py:87
  289.5 31.6 %all_to_all.5 = bf16[8,256,224]{1,2,0:T(8,128)(2,1)S(1)} all-to-all(bf16[8,256,224]{1,2,0:T(8,128)(2,1)S(1)} %bitcast.42), channel_id=1, replica_groups=mesh['groups'=2,'ctx'=32,'tp'=8] {'tp'}, dimensions={0} | all-to-all | bytes 1835008 | tf_op jit(solution)/shard_map/all_to_all | solution.py:30
  (26 shorter events, 5.0 us)
Async XLA Ops:
  6.5 276.9 %copy-start = (bf16[2048,224]{0,1:T(8,128)(2,1)S(1)}, bf16[2048,224]{0,1:T(8,128)(2,1)}, u32[]{:S(2)}) copy-start(bf16[2048,224]{0,1:T(8,128)(2,1)} %param.15) | copy-start | bytes 2752516
  6.6 113.9 %all-gather.9.cloned.1.call-start = ((), (), s32[]{:S(2)}) async-start(), calls=%async_computation.3 | async-start | bytes 4325376 | tf_op jit(solution)/shard_map/all_gather | solution.py:15
  9.0 183.7 %all-gather.5.cloned.1.call-start = ((), (), s32[]{:S(2)}) async-start(), calls=%async_computation.1 | async-start | bytes 2703360 | tf_op jit(solution)/shard_map/all_gather | solution.py:70
  12.4 271.0 %all-gather.7.cloned.1.call-start = ((), (), s32[]{:S(2)}) async-start(), calls=%async_computation.2 | async-start | bytes 8650752 | tf_op jit(solution)/shard_map/all_gather | solution.py:88
  140.0 2.1 copy-start.1
  198.7 2.8 copy-start.2
Sparse Core Ops, SparseCore 0:
  9.5 110.9 all-gather.8
  122.6 70.1 all-gather.4
  206.4 76.9 all-gather.6
where the time goes:
time: 329 us; the launch traced here: 328 us
  waiting for transfers between devices  172 us (52%)
  blocking collectives  89.1 us (27%)
  local copies, waits for them, and re-layouts  27.1 us (8%)
  matrix products  17.2 us (5%)
  between operations  14 us (4%)
  other arithmetic  8.72 us (3%)
    all_gather x1, waiting for transfers between devices, on_device(): lax.all_gather(rows_out, 'ctx', axis=0, tiled=True)  77.1 us
    unnamed x1, blocking collectives  57.5 us
    all_gather x1, waiting for transfers between devices, on_device(): key_part = lax.all_gather(key_rows, 'ctx', axis=0, tiled=True)  49.6 us
    all_gather x1, waiting for transfers between devices, gather_together(): lines, at, gathered = (lax.all_gather(flat, axis), 0, [])  45.3 us
    all_to_all x1, blocking collectives, sent_and_summed(): lax.all_to_all(blocks, axis, split_axis=0, concat_axis=0, tiled=True)  31.6 us
  transfers between devices with their start and end apart: 3, of which 3 were waited for; matrix products, arithmetic and copies ran while one was open for 9% of the time, Pallas kernels for 0%

commit v1 on v0

--- a/solution.py
+++ b/solution.py
@@ -67,7 +67,10 @@
     )
     query_pos = jnp.repeat(positions, head_count)
     row_total = tok_count * head_count
-    key_part = lax.all_gather(key_rows, "ctx", axis=0, tiled=True)
+    count = lax.axis_size("ctx")
+    pieces = jnp.stack([key_rows for _ in range(count)])
+    pieces = lax.all_to_all(pieces, "ctx", split_axis=0, concat_axis=0)
+    key_part = jnp.concatenate(pieces, axis=0)
     key_pos = lax.all_gather(positions, "ctx", axis=0, tiled=True)
     run_max = jnp.full((row_total,), -1e30, jnp.float32)
     scores = (

time: 329 us -> 376 us (1.14)
  waiting for transfers between devices: 172 us -> 84.1 us
  blocking collectives: 89.1 us -> 176 us
  starting transfers between devices: 0.13 us -> 46.2 us
    unnamed x1, blocking collectives: 57.5 us -> 145 us
    all_gather x1 -> x0, waiting for transfers between devices: 49.6 us -> none  [on_device(): key_part = lax.all_gather(key_rows, 'ctx', axis=0, tiled=True)]
    all_to_all x0 -> x1, starting transfers between devices: none -> 46.2 us  [on_device(): pieces = lax.all_to_all(pieces, 'ctx', split_axis=0, concat_axis=0)]
    all_gather x1, waiting for transfers between devices: 45.3 us -> 0.02 us  [gather_together(): lines, at, gathered = (lax.all_gather(flat, axis), 0, [])]
    all_gather x1, waiting for transfers between devices: 77.1 us -> 84 us  [on_device(): lax.all_gather(rows_out, 'ctx', axis=0, tiled=True)]
  transfers between devices with their start and end apart: 3 -> 3, of which waited for: 3 -> 1; matrix products, arithmetic and copies ran while one was open for 9% -> 8% of each run, Pallas kernels for 0% -> 0%
where the time goes in v1:
time: 376 us; the launch traced here: 375 us
  blocking collectives  176 us (47%)
  waiting for transfers between devices  84.1 us (22%)
  starting transfers between devices  46.2 us (12%)
  local copies, waits for them, and re-layouts  26.7 us (7%)
  matrix products  18.9 us (5%)
  between operations  14.3 us (4%)
  other arithmetic  8.09 us (2%)
    unnamed x1, blocking collectives  145 us
    all_gather x1, waiting for transfers between devices, on_device(): lax.all_gather(rows_out, 'ctx', axis=0, tiled=True)  84 us
    all_to_all x1, starting transfers between devices, on_device(): pieces = lax.all_to_all(pieces, 'ctx', split_axis=0, concat_axis=0)  46.2 us
    all_to_all x1, blocking collectives, sent_and_summed(): lax.all_to_all(blocks, axis, split_axis=0, concat_axis=0, tiled=True)  31.6 us
  transfers between devices with their start and end apart: 3, of which 1 were waited for; matrix products, arithmetic and copies ran while one was open for 8% of the time, Pallas kernels for 0%

profile of v1, /device:TPU:65, one launch (start us, length us, event | category | flops | bytes accessed | tf_op | source)
XLA Modules:
  0.0 374.8 jit_solution(17312169179815345282)
XLA Ops:
  6.6 0.9 copy.33
  7.5 1.5 pad_maximum_fusion.1
  9.7 1.0 fusion.20
  10.7 0.9 pad_maximum_fusion.2
  11.6 1.9 stack.2
  13.6 46.2 %all-to-all-start = ((bf16[32,64,576]{2,1,0:T(8,128)(2,1)}), bf16[32,64,576]{2,1,0:T(8,128)(2,1)}, u32[]{:S(2)}, u32[]{:S(2)}) async-start(bf16[32,64,576]{2,1,0:T(8,128)(2,1)} %stack.2), calls=%async_computation | async-start | bytes 5242880 | tf_op jit(solution)/shard_map/all_to_all | solution.py:72
  60.2 1.3 dynamic-slice
  62.4 144.9 %all-reduce = s32[2048]{0:T(1024)S(1)} all-reduce(s32[2048]{0:T(1024)S(1)} %dynamic-update-slice), channel_id=1, replica_groups=mesh['groups'=2,'ctx'=32,'tp'=8] {'ctx'}, use_global_device_ids=true, to_apply=%add | all-reduce | flops 2048 | bytes 16384
  207.7 5.6 %reshape.129 = bf16[32,65536]{1,0:T(8,128)(2,1)} reshape(bf16[2097152]{0:T(1024)(128)(2,1)} %all-gather.6.cloned.1.call-done) | data formatting | bytes 8388608 | tf_op jit(solution)/shard_map/all_gather | solution.py:15
  213.2 4.4 %fusion.25 = (bf16[32,32768]{1,0:T(8,128)(2,1)}, bf16[4,8,256,128]{3,1,2,0:T(8,128)(2,1)}) fusion(bf16[32,65536]{1,0:T(8,128)(2,1)} %reshape.129), kind=kLoop, calls=%fused_computation.44 | loop fusion | bytes 8388608 | tf_op jit(solution)/shard_map/slice | solution.py:17
  217.7 3.3 reshape.120
  221.0 2.3 copy.20
  223.3 2.5 reshape.121
  225.9 1.4 fusion.6
  227.5 1.8 copy.24
  230.4 5.9 %fusion = (f32[1024]{0:T(1024)S(1)}, f32[1024,2048]{1,0:T(8,128)S(1)}) fusion(s32[2048]{0:T(1024)S(1)} %all-reduce, s32[1024]{0:T(1024)S(1)} %le.16, bf16[1024,576]{1,0:T(8,128)(2,1)} %bitcast.44, bf16[2048,576]{1,0:T(8,128)(2,1)} %bitcast.7), kind=kOutput, calls=%fused_computation.2 | convolution fusion | flops 2424306688 | bytes 11943936 | tf_op jit(solution)/shard_map/rk,sk->rs/dot_general | solution.py:77
  236.3 2.8 fusion.1
  239.1 4.1 %divide_convert_fusion = bf16[1024,512]{1,0:T(8,128)(2,1)S(1)} fusion(f32[1024]{0:T(1024)S(1)} %fusion.1, bf16[2048,576]{1,0:T(8,128)(2,1)} %bitcast.7, f32[1024,2048]{1,0:T(8,128)S(1)} %get-tuple-element.16, f32[1024]{0:T(1024)S(1)} %broadcast_maximum_fusion, s32[2048]{0:T(1024)S(1)} %all-reduce, s32[1024]{0:T(1024)S(1)} %le.16), kind=kOutput, calls=%fused_computation.9 | convolution fusion | flops 2159017984 | bytes 11554816 | tf_op jit(solution)/shard_map/dot_general | solution.py:84
  243.2 1.4 fusion.7
  244.6 0.8 copy.48
  245.5 84.0 %all-gather.4.cloned.1.call-done = bf16[2048,2048]{1,0:T(8,128)(2,1)} async-done(((bf16[64,2048]{1,0:T(8,128)(2,1)}), bf16[2048,2048]{1,0:T(8,128)(2,1)}) %all-gather.4.cloned.1.call-update) | async-done | bytes 8388624 | tf_op jit(solution)/shard_map/all_gather | solution.py:91
  329.5 6.0 %convolution_convert_fusion = bf16[2048,224]{0,1:T(8,128)(2,1)S(1)} fusion(bf16[2048,2048]{1,0:T(8,128)(2,1)} %all-gather.4.cloned.1.call-done, bf16[2048,224]{0,1:T(8,128)(2,1)S(1)} %copy-done), kind=kOutput, calls=%fused_computation.6 | convolution fusion | flops 1879506944 | bytes 10223616 | tf_op jit(solution)/shard_map/dot_general | solution.py:90
  335.6 31.6 %all_to_all.10 = bf16[8,256,224]{1,2,0:T(8,128)(2,1)S(1)} all-to-all(bf16[8,256,224]{1,2,0:T(8,128)(2,1)S(1)} %bitcast.43), channel_id=1, replica_groups=mesh['groups'=2,'ctx'=32,'tp'=8] {'tp'}, dimensions={0} | all-to-all | bytes 1835008 | tf_op jit(solution)/shard_map/all_to_all | solution.py:30
  367.2 0.8 reduce_sum.22
  (28 shorter events, 3.2 us)
Async XLA Ops:
  6.5 322.9 %copy-start = (bf16[2048,224]{0,1:T(8,128)(2,1)S(1)}, bf16[2048,224]{0,1:T(8,128)(2,1)}, u32[]{:S(2)}) copy-start(bf16[2048,224]{0,1:T(8,128)(2,1)} %param.15) | copy-start | bytes 2752516
  6.6 201.1 %all-gather.6.cloned.1.call-start = ((), (), s32[]{:S(2)}) async-start(), calls=%async_computation.3 | async-start | bytes 4325376 | tf_op jit(solution)/shard_map/all_gather | solution.py:15
  13.6 46.2 %copy-start.3 = (s32[64]{0:T(128)S(1)}, s32[64]{0:T(128)}, u32[]{:S(2)}) copy-start(s32[64]{0:T(128)} %param.12) | copy-start | bytes 772
  13.6 46.4 %copy-start.2 = (bf16[64,1024]{1,0:T(8,128)(2,1)S(1)}, bf16[64,1024]{1,0:T(8,128)(2,1)}, u32[]{:S(2)}) copy-start(bf16[64,1024]{1,0:T(8,128)(2,1)} %param.9) | copy-start | bytes 393220
  13.6 216.8 %all-to-all-start = ((bf16[32,64,576]{2,1,0:T(8,128)(2,1)}), bf16[32,64,576]{2,1,0:T(8,128)(2,1)}, u32[]{:S(2)}, u32[]{:S(2)}) async-start(bf16[32,64,576]{2,1,0:T(8,128)(2,1)} %stack.2), calls=%async_computation | async-start | bytes 5242880 | tf_op jit(solution)/shard_map/all_to_all | solution.py:72
  59.7 269.7 %all-gather.4.cloned.1.call-start = ((), (), s32[]{:S(2)}) async-start(), calls=%async_computation.2 | async-start | bytes 8650752 | tf_op jit(solution)/shard_map/all_gather | solution.py:91
  227.2 2.1 copy-start.1
Sparse Core Ops, SparseCore 0:
  9.5 177.9 all-gather.5
  245.6 83.8 all-gather.3

commit v2 on v0

--- a/solution.py
+++ b/solution.py
@@ -1,7 +1,18 @@
+import functools
 import jax
 import jax.numpy as jnp
 from jax import lax
 from jax.sharding import PartitionSpec as P
+
+
+def detail_core(x_part, across):
+    n_dev_all = lax.psum(1, across)
+    tray = [n_dev_all if p == 0 else 1 for p in range(x_part.ndim)]
+    now = lax.all_to_all(jnp.tile(x_part, tray), across, concat_axis=0, tiled=True, split_axis=0)
+    return now
+
+
+push_the_counts = functools.partial(detail_core, across="ctx")
 
 
 def laid_out(blocks, dim):
@@ -84,11 +95,7 @@
     o_lat = (added / new_sum[:, None]).astype(jnp.bfloat16).reshape(tok_count, head_count, latent)
     head_out = jnp.einsum("thl,hlv->thv", o_lat, up_value, preferred_element_type=jnp.float32)
     rows_out = head_out.astype(jnp.bfloat16).reshape(tok_count, -1)
-    partial_value = jnp.dot(
-        lax.all_gather(rows_out, "ctx", axis=0, tiled=True),
-        w_out,
-        preferred_element_type=jnp.float32,
-    )
+    partial_value = jnp.dot(push_the_counts(rows_out), w_out, preferred_element_type=jnp.float32)
     summed = sent_and_summed(partial_value.astype(jnp.bfloat16), "tp", 0)
     return summed.astype(jnp.bfloat16)
 

time: 329 us -> 627 us (1.91)
  blocking collectives: 89.1 us -> 467 us
  waiting for transfers between devices: 172 us -> 95.2 us
    all_to_all x0 -> x1, blocking collectives: none -> 378 us  [detail_core(): lax.all_to_all(jnp.tile(x_part, tray), across, concat_axis=0, tiled=True,...]
    all_gather x1 -> x0, waiting for transfers between devices: 77.1 us -> none  [on_device(): lax.all_gather(rows_out, 'ctx', axis=0, tiled=True)]
  transfers between devices with their start and end apart: 3 -> 2, of which waited for: 3 -> 2; matrix products, arithmetic and copies ran while one was open for 9% -> 5% of each run, Pallas kernels for 0% -> 0%
where the time goes in v2:
time: 627 us; the launch traced here: 626 us
  blocking collectives  467 us (74%)
  waiting for transfers between devices  95.2 us (15%)
  local copies, waits for them, and re-layouts  27.4 us (4%)
  between operations  14.3 us (2%)
  matrix products  13.8 us (2%)
  other arithmetic  8.73 us (1%)
    all_to_all x1, blocking collectives, detail_core(): lax.all_to_all(jnp.tile(x_part, tray), across, concat_axis=0, tiled=True,...  378 us
    unnamed x1, blocking collectives  57.4 us
    all_gather x1, waiting for transfers between devices, on_device(): key_part = lax.all_gather(key_rows, 'ctx', axis=0, tiled=True)  49.7 us
    all_gather x1, waiting for transfers between devices, gather_together(): lines, at, gathered = (lax.all_gather(flat, axis), 0, [])  45.4 us
    all_to_all x1, blocking collectives, sent_and_summed(): lax.all_to_all(blocks, axis, split_axis=0, concat_axis=0, tiled=True)  31 us
  transfers between devices with their start and end apart: 2, of which 2 were waited for; matrix products, arithmetic and copies ran while one was open for 5% of the time, Pallas kernels for 0%

profile of v2, /device:TPU:65, one launch (start us, length us, event | category | flops | bytes accessed | tf_op | source)
XLA Modules:
  0.0 626.0 jit_solution(11325682776673063179)
XLA Ops:
  6.6 0.9 copy.33
  7.5 1.5 pad_maximum_fusion.1
  9.8 1.0 fusion.20
  10.8 1.6 pad_maximum_fusion.2
  12.4 1.3 dynamic-slice
  15.3 57.4 %all-reduce = s32[2048]{0:T(1024)S(1)} all-reduce(s32[2048]{0:T(1024)S(1)} %dynamic-update-slice), channel_id=1, replica_groups=mesh['groups'=2,'ctx'=32,'tp'=8] {'ctx'}, use_global_device_ids=true, to_apply=%add | all-reduce | flops 2048 | bytes 16384
  73.5 1.1 reshape.122
  75.0 45.4 %all-gather.6.cloned.1.call-done = bf16[2097152]{0:T(1024)(128)(2,1)} async-done(((bf16[65536]{0:T(1024)(128)(2,1)}), bf16[2097152]{0:T(1024)(128)(2,1)}) %all-gather.6.cloned.1.call-update) | async-done | bytes 4194320 | tf_op jit(solution)/shard_map/all_gather | solution.py:26
  120.4 5.5 reshape.126
  126.0 4.4 fusion.25
  130.4 3.3 reshape.119
  133.7 2.3 copy.20
  136.0 2.5 reshape.120
  138.6 1.4 fusion.6
  140.2 1.8 copy.24
  143.1 49.7 %all-gather.4.cloned.1.call-done = bf16[2048,576]{1,0:T(8,128)(2,1)} async-done(((bf16[64,576]{1,0:T(8,128)(2,1)}), bf16[2048,576]{1,0:T(8,128)(2,1)}) %all-gather.4.cloned.1.call-update) | async-done | bytes 2359312 | tf_op jit(solution)/shard_map/all_gather | solution.py:81
  192.8 5.9 fusion
  198.7 2.8 fusion.1
  201.5 2.5 divide_convert_fusion
  204.0 1.4 fusion.7
  205.5 1.1 tile.9
  206.5 378.2 %all_to_all.14 = bf16[32,64,2048]{2,1,0:T(8,128)(2,1)S(1)} all-to-all(bf16[32,64,2048]{2,1,0:T(8,128)(2,1)S(1)} %tile.9), channel_id=1, replica_groups=mesh['groups'=2,'ctx'=32,'tp'=8] {'ctx'}, dimensions={0} | all-to-all | bytes 16777216 | tf_op jit(solution)/shard_map/all_to_all | solution.py:11
  584.7 2.6 convolution_convert_fusion
  587.4 31.0 %all_to_all.15 = bf16[8,256,224]{1,2,0:T(8,128)(2,1)S(1)} all-to-all(bf16[8,256,224]{1,2,0:T(8,128)(2,1)S(1)} %bitcast.44), channel_id=1, replica_groups=mesh['groups'=2,'ctx'=32,'tp'=8] {'tp'}, dimensions={0} | all-to-all | bytes 1835008 | tf_op jit(solution)/shard_map/all_to_all | solution.py:41
  (25 shorter events, 5.0 us)
Async XLA Ops:
  6.5 578.2 %copy-start = (bf16[2048,224]{0,1:T(8,128)(2,1)S(1)}, bf16[2048,224]{0,1:T(8,128)(2,1)}, u32[]{:S(2)}) copy-start(bf16[2048,224]{0,1:T(8,128)(2,1)} %param.15) | copy-start | bytes 2752516
  6.6 113.9 %all-gather.6.cloned.1.call-start = ((), (), s32[]{:S(2)}) async-start(), calls=%async_computation.3 | async-start | bytes 4325376 | tf_op jit(solution)/shard_map/all_gather | solution.py:26
  9.1 183.7 %all-gather.4.cloned.1.call-start = ((), (), s32[]{:S(2)}) async-start(), calls=%async_computation.2 | async-start | bytes 2703360 | tf_op jit(solution)/shard_map/all_gather | solution.py:81
  140.0 2.1 copy-start.1
  198.7 2.8 copy-start.2
Sparse Core Ops, SparseCore 0:
  9.5 110.8 all-gather.5
  122.6 70.1 all-gather.3
